TPU v7x, 32 devices: a whole 2x2x4 slice. The times are simulated.
32 devices in a mesh: dp: 8 (over z, x), rep: 4 (over y, core).
Axes of the slice: x: 2, y: 2, z: 4, core: 2. Of those that a mesh axis runs over, the one named last changes fastest.
Arguments:
- tokens: bfloat16 [8192, 2048], P(('rep', 'dp')), parts along dimension 0, may hold values from -12 to 12
- router: bfloat16 [8192, 8], P('rep'), parts along dimension 0, may hold values from -12 to 12
- w_gate: bfloat16 [8, 2048, 768], P('dp'), may hold values from -0.125 to 0.125
- w_up: bfloat16 [8, 2048, 768], P('dp'), may hold values from -0.125 to 0.125
- w_down: bfloat16 [8, 768, 2048], P('dp'), may hold values from -0.21875 to 0.21875
- picks: int32 [32, 32], P(('rep', 'dp')), parts along dimension 0, may hold values from 0 to 2047, as said below
Outputs:
- combined: bfloat16 [8192, 2048], P(('rep', 'dp')), parts along dimension 0
There are 4 independent parts, one for each index of `rep`. A program takes and returns all parts, laid end to end along the dimension named above; an argument that names none is the same for every part. Nothing has to cross between parts.
Inputs may be any that keep to these rules, and one draw needn't show every extreme that they name: `picks`: row e holds 32 different tokens taken by expert e, sorted by the device that holds them (256 tokens each, in order); at most 6 of them lie among one device's tokens, and in every row exactly 6 lie among some device's tokens.
All inputs are finite; a program needn't handle non-finite values.
Results may differ from a plain program's by a relative error of at most 0.0062.
Values may be sent and summed in bfloat16 or wider, within the bound.
A program may use at most 64 MiB of HBM per device.

v0:
```python
import functools

import jax
import jax.numpy as jnp
from jax import lax
from jax.experimental import pallas as pl
from jax.experimental.pallas import tpu as pltpu
from jax.sharding import PartitionSpec as P

MESH = pl.DeviceIdType.MESH
MOST = 6
SUB = 8
PARTS = 4
FOLD = 3
F32 = jnp.float32
BF16 = jnp.bfloat16


def mm(a, b):
    return jnp.dot(a, b, preferred_element_type=F32)


def mm_t(a, b):
    return lax.dot_general(a, b, (((0,), (0,)), ((), ())), preferred_element_type=F32)


def kernel(
    n, tokens, router, w_gate, w_up, w_down, picks, out,
    tok, rout, wg, wu, wd, pk_own, pk_out, pk_in, x_out, x_in, y_out, y_in,
    load_sem, wg_sem, wu_sem,
    pk_send, pk_recv, x_send, x_recv, y_send, y_recv,
):
    me = lax.axis_index("dp")
    tok_dev, width = tok.shape
    cols = width // PARTS
    piece = cols // (FOLD + 1)
    wide = FOLD * piece
    cap = picks.shape[1]
    lanes = pk_out.shape[1]
    rows = n * SUB
    experts = rout.shape[0]

    def span(k):
        return pl.ds(k * cols, cols)

    def front(k):
        return pl.ds(k * cols, wide)

    def back(k):
        return pl.ds(k * cols + wide, piece)

    def fold(matrices, x):
        return jnp.concatenate([mm(m, x) for m in matrices], axis=1)

    def unfold(dot, matrices, x):
        return sum(dot(m, x[:, j * piece : (j + 1) * piece]) for j, m in enumerate(matrices))

    load_tok = pltpu.make_async_copy(tokens, tok, load_sem.at[0])
    load_rout = pltpu.make_async_copy(router, rout, load_sem.at[1])
    load_pk = pltpu.make_async_copy(picks, pk_own, load_sem.at[3])
    load_wd = pltpu.make_async_copy(w_down.at[0], wd, load_sem.at[2])
    load_wg = [
        pltpu.make_async_copy(w_gate.at[0, span(k)], wg.at[span(k)], wg_sem.at[k])
        for k in range(PARTS)
    ]
    load_wu = [
        pltpu.make_async_copy(w_up.at[0, span(k)], wu.at[span(k)], wu_sem.at[k])
        for k in range(PARTS)
    ]

    barrier = pltpu.get_barrier_semaphore()
    peers = [lax.rem(me + i, n) for i in range(1, n)]
    for peer in peers:
        pl.semaphore_signal(barrier, inc=1, device_id={"dp": peer}, device_id_type=MESH)
    load_pk.start()
    load_tok.start()
    load_rout.start()
    for k in range(PARTS):
        load_wg[k].start()
        load_wu[k].start()
    load_wd.start()

    pk_out[...] = jnp.full((SUB, lanes), 1 << 30, jnp.int32)
    load_pk.wait()
    pk_out[:, pl.ds(0, cap)] = jnp.broadcast_to(pk_own[...], (SUB, cap))
    pk_in[me] = pk_out[...]
    pl.semaphore_wait(barrier, n - 1)

    def send(src, dst, send_sem, recv_sem, peer):
        return pltpu.make_async_remote_copy(
            src_ref=src, dst_ref=dst, send_sem=send_sem, recv_sem=recv_sem,
            device_id={"dp": peer}, device_id_type=MESH,
        )

    pk_copies = [
        send(pk_out, pk_in.at[me], pk_send.at[i], pk_recv.at[i], peer)
        for i, peer in enumerate(peers)
    ]
    for copy in pk_copies:
        copy.start()

    row_sub = lax.broadcasted_iota(jnp.int32, (rows, 1), 0) % SUB
    r_i = lax.broadcasted_iota(jnp.int32, (rows, rows), 0)
    q_i = lax.broadcasted_iota(jnp.int32, (rows, rows), 1)
    same = r_i // SUB == q_i // SUB
    spread = []
    gather = []
    for k in range(FOLD):
        a = (r_i % SUB == k) & (q_i % SUB == MOST)
        b = (r_i % SUB == FOLD + k) & (q_i % SUB == MOST + 1)
        spread.append(jnp.where(same & (a | b), 1.0, 0.0).astype(BF16))
        a = (q_i % SUB == k) & (r_i % SUB == MOST)
        b = (q_i % SUB == FOLD + k) & (r_i % SUB == MOST + 1)
        gather.append(jnp.where(same & (a | b), 1.0, 0.0).astype(BF16))
    load_tok.wait()
    for copy in pk_copies:
        copy.wait_recv()

    pk = pk_in[...].reshape(rows, lanes)
    low = me * tok_dev
    mine = (pk >= low) & (pk < low + tok_dev)
    start = jnp.sum(jnp.where(pk < low, 1.0, 0.0), axis=1, keepdims=True).astype(jnp.int32)
    slot = lax.broadcasted_iota(jnp.int32, (rows, lanes), 1) - start
    place = (pk - low + 1).astype(F32)
    token_at = lax.broadcasted_iota(jnp.int32, (rows, tok_dev), 1).astype(F32) + 1.0

    def onehot(slot_of_row):
        at = jnp.sum(jnp.where(mine & (slot == slot_of_row), place, 0.0), axis=1, keepdims=True)
        return jnp.where(token_at == at, 1.0, 0.0).astype(BF16)

    main = onehot(row_sub)
    tails = [
        onehot(jnp.where(row_sub == MOST, k, jnp.where(row_sub == MOST + 1, FOLD + k, -1)))
        for k in range(FOLD)
    ]

    x_copies = [
        [
            send(x_out.at[k, peer], x_in.at[k, me], x_send.at[k, i], x_recv.at[k, i], peer)
            for i, peer in enumerate(peers)
        ]
        for k in range(PARTS)
    ]
    for k in range(PARTS):
        block = mm(main, tok[:, front(k)]) + fold(tails, tok[:, back(k)])
        x_out[k] = block.astype(BF16).reshape(n, SUB, wide)
        x_in[k, me] = x_out[k, me]
        for copy in x_copies[k]:
            copy.start()

    gate_act = up_act = logits = None

    def total(a, b):
        return b if a is None else a + b

    def step(x, k):
        dims = (((1,), (1,)), ((), ()))
        return (
            total(gate_act, mm(x, wg[span(k)])),
            total(up_act, mm(x, wu[span(k)])),
            total(logits, lax.dot_general(x, rout[:, span(k)], dims, preferred_element_type=F32)),
        )

    load_rout.wait()
    for k in range(PARTS):
        load_wg[k].wait()
        load_wu[k].wait()
        for copy in x_copies[k]:
            copy.wait_recv()
        x = x_in[k].reshape(rows, wide)
        x = jnp.concatenate([x, unfold(mm, spread, x).astype(BF16)], axis=1)
        gate_act, up_act, logits = step(x, k)

    e = jnp.exp(logits - jnp.max(logits, axis=1, keepdims=True))
    own = lax.broadcasted_iota(jnp.int32, (rows, experts), 1) == me
    share = jnp.sum(jnp.where(own, e, 0.0), axis=1, keepdims=True) / jnp.sum(e, axis=1, keepdims=True)
    gates = (experts * share).astype(BF16).astype(F32)
    silu = gate_act / (1.0 + jnp.exp(-gate_act))
    hidden = (gates * silu * up_act).astype(BF16)

    load_wd.wait()
    y_copies = [
        [
            send(y_out.at[k, peer], y_in.at[k, me], y_send.at[k, i], y_recv.at[k, i], peer)
            for i, peer in enumerate(peers)
        ]
        for k in range(PARTS)
    ]
    for k in range(PARTS):
        block = mm(hidden, wd[:, span(k)])
        block = jnp.where(row_sub < MOST, block[:, :wide], fold(gather, block[:, wide:].astype(BF16)))
        y_out[k] = block.astype(BF16).reshape(n, SUB, wide)
        y_in[k, me] = y_out[k, me]
        for copy in y_copies[k]:
            copy.start()

    for k in range(PARTS):
        for copy in y_copies[k]:
            copy.wait_recv()
        y = y_in[k].reshape(rows, wide)
        out[:, front(k)] = mm_t(main, y).astype(BF16)
        out[:, back(k)] = unfold(mm_t, tails, y).astype(BF16)
    for copies in [pk_copies] + x_copies + y_copies:
        for copy in copies:
            copy.wait_send()


def body(tokens, router, w_gate, w_up, w_down, picks):
    n = lax.axis_size("dp")
    tok_dev, width = tokens.shape
    hidden = w_gate.shape[2]
    wide = width // PARTS * FOLD // (FOLD + 1)
    cap = picks.shape[1]
    lanes = -(-cap // 128) * 128
    experts = router.shape[1]
    dma = pltpu.SemaphoreType.DMA
    block = pltpu.VMEM((PARTS, n, SUB, wide), BF16)
    return pl.pallas_call(
        functools.partial(kernel, n),
        out_shape=pltpu.VMEM((tok_dev, width), BF16),
        in_specs=[pl.BlockSpec(memory_space=pl.ANY)] * 6,
        out_specs=pl.BlockSpec(memory_space=pltpu.VMEM),
        scratch_shapes=[
            pltpu.VMEM((tok_dev, width), BF16),
            pltpu.VMEM((experts, width), BF16),
            pltpu.VMEM((width, hidden), BF16),
            pltpu.VMEM((width, hidden), BF16),
            pltpu.VMEM((hidden, width), BF16),
            pltpu.VMEM((1, cap), jnp.int32),
            pltpu.VMEM((SUB, lanes), jnp.int32),
            pltpu.VMEM((n, SUB, lanes), jnp.int32),
            block, block, block, block,
            dma((4,)), dma((PARTS,)), dma((PARTS,)),
            dma((n - 1,)), dma((n - 1,)),
            dma((PARTS, n - 1)), dma((PARTS, n - 1)),
            dma((PARTS, n - 1)), dma((PARTS, n - 1)),
        ],
        compiler_params=pltpu.CompilerParams(collective_id=0, has_side_effects=True),
    )(tokens, router.T, w_gate, w_up, w_down, picks)


def solution(mesh):
    return jax.shard_map(
        body,
        mesh=mesh,
        in_specs=(
            P(("rep", "dp"), None),
            P("rep", None),
            P("dp", None, None),
            P("dp", None, None),
            P("dp", None, None),
            P(("rep", "dp"), None),
        ),
        out_specs=P(("rep", "dp"), None),
        check_vma=False,
    )
```

profile of v0, /device:TPU:0, one launch (start us, length us, event | category | flops | bytes accessed | tf_op | source)
XLA Modules:
  0.0 24.5 jit_solution(17927580820031950739)
XLA Ops:
  0.0 23.5 %shard_map.64 = bf16[256,2048]{1,0:T(8,128)(2,1)S(1)} custom-call(bf16[256,2048]{1,0:T(8,128)(2,1)} %tokens.1, bf16[8,2048]{1,0:T(8,128)(2,1)} %bitcast.1, bf16[1,2048,768]{2,1,0:T(8,128)(2,1)} %w_gate.1, bf16[1,2048,768]{2,1,0:T(8,128)(2,1)} %w_up.1, bf16[1,768,2048]{2,1,0:T(8,128)(2,1)} %w_down.1, s32[1,32]{1,0:T(1,128)} %picks.1), custom_call_target="tpu_custom_call" | custom-call | tf_op jit(solution)/shard_map/pallas_call | solution.py:218
  23.5 1.0 %copy.8 = bf16[256,2048]{1,0:T(8,128)(2,1)} copy(bf16[256,2048]{1,0:T(8,128)(2,1)S(1)} %shard_map.64) | data formatting | bytes 2097152
where the time goes:
time: 24.6 us; the launch traced here: 24.5 us
  Pallas kernels  23.5 us (96%)
  local copies, waits for them, and re-layouts  0.97 us (4%)
    pallas_call x1, Pallas kernels, body(): pl.pallas_call(functools.partial(kernel, n), out_shape=pltpu.VMEM((tok_de...  23.5 us
    unnamed x1, local copies, waits for them, and re-layouts  0.97 us

commit v1 on v0

--- a/solution.py
+++ b/solution.py
@@ -25,7 +25,7 @@
 
 
 def kernel(
-    n, tokens, router, w_gate, w_up, w_down, picks, out,
+    n, first_half, tokens, router, w_gate, w_up, w_down, picks, out,
     tok, rout, wg, wu, wd, pk_own, pk_out, pk_in, x_out, x_in, y_out, y_in,
     load_sem, wg_sem, wu_sem,
     pk_send, pk_recv, x_send, x_recv, y_send, y_recv,
@@ -69,7 +69,7 @@
     ]
 
     barrier = pltpu.get_barrier_semaphore()
-    peers = [lax.rem(me + i, n) for i in range(1, n)]
+    peers = [n - 1 - j - (n - 1 - j <= me).astype(jnp.int32) for j in range(n - 1)]
     for peer in peers:
         pl.semaphore_signal(barrier, inc=1, device_id={"dp": peer}, device_id_type=MESH)
     load_pk.start()
@@ -93,11 +93,15 @@
         )
 
     pk_copies = [
-        send(pk_out, pk_in.at[me], pk_send.at[i], pk_recv.at[i], peer)
+        send(pk_out, pk_in.at[me], pk_send.at[peer], pk_recv.at[me], peer)
         for i, peer in enumerate(peers)
     ]
     for copy in pk_copies:
         copy.start()
+    pk_waits = [
+        send(pk_out, pk_in.at[peer], pk_send.at[peer], pk_recv.at[peer], peer)
+        for i, peer in enumerate(peers)
+    ]
 
     row_sub = lax.broadcasted_iota(jnp.int32, (rows, 1), 0) % SUB
     r_i = lax.broadcasted_iota(jnp.int32, (rows, rows), 0)
@@ -113,40 +117,69 @@
         b = (q_i % SUB == FOLD + k) & (r_i % SUB == MOST + 1)
         gather.append(jnp.where(same & (a | b), 1.0, 0.0).astype(BF16))
     load_tok.wait()
-    for copy in pk_copies:
-        copy.wait_recv()
-
-    pk = pk_in[...].reshape(rows, lanes)
+
     low = me * tok_dev
-    mine = (pk >= low) & (pk < low + tok_dev)
-    start = jnp.sum(jnp.where(pk < low, 1.0, 0.0), axis=1, keepdims=True).astype(jnp.int32)
-    slot = lax.broadcasted_iota(jnp.int32, (rows, lanes), 1) - start
-    place = (pk - low + 1).astype(F32)
-    token_at = lax.broadcasted_iota(jnp.int32, (rows, tok_dev), 1).astype(F32) + 1.0
-
-    def onehot(slot_of_row):
-        at = jnp.sum(jnp.where(mine & (slot == slot_of_row), place, 0.0), axis=1, keepdims=True)
-        return jnp.where(token_at == at, 1.0, 0.0).astype(BF16)
-
-    main = onehot(row_sub)
-    tails = [
-        onehot(jnp.where(row_sub == MOST, k, jnp.where(row_sub == MOST + 1, FOLD + k, -1)))
-        for k in range(FOLD)
-    ]
+
+    def choose(pk):
+        count = pk.shape[0]
+        mine = (pk >= low) & (pk < low + tok_dev)
+        start = jnp.sum(jnp.where(pk < low, 1.0, 0.0), axis=1, keepdims=True).astype(jnp.int32)
+        slot = lax.broadcasted_iota(jnp.int32, (count, lanes), 1) - start
+        place = (pk - low + 1).astype(F32)
+        token_at = lax.broadcasted_iota(jnp.int32, (count, tok_dev), 1).astype(F32) + 1.0
+        sub = lax.broadcasted_iota(jnp.int32, (count, 1), 0) % SUB
+
+        def onehot(slot_of_row):
+            at = jnp.sum(jnp.where(mine & (slot == slot_of_row), place, 0.0), axis=1, keepdims=True)
+            return jnp.where(token_at == at, 1.0, 0.0).astype(BF16)
+
+        return [onehot(sub)] + [
+            onehot(jnp.where(sub == MOST, k, jnp.where(sub == MOST + 1, FOLD + k, -1)))
+            for k in range(FOLD)
+        ]
 
     x_copies = [
         [
-            send(x_out.at[k, peer], x_in.at[k, me], x_send.at[k, i], x_recv.at[k, i], peer)
-            for i, peer in enumerate(peers)
-        ]
-        for k in range(PARTS)
-    ]
-    for k in range(PARTS):
-        block = mm(main, tok[:, front(k)]) + fold(tails, tok[:, back(k)])
-        x_out[k] = block.astype(BF16).reshape(n, SUB, wide)
+            send(x_out.at[k, peer], x_in.at[k, me], x_send.at[k, peer], x_recv.at[k, me], peer)
+            for i, peer in enumerate(peers)
+        ]
+        for k in range(PARTS)
+    ]
+    x_waits = [
+        [
+            send(x_out.at[k, peer], x_in.at[k, peer], x_send.at[k, peer], x_recv.at[k, peer], peer)
+            for i, peer in enumerate(peers)
+        ]
+        for k in range(PARTS)
+    ]
+    turn = n - first_half - 1
+    chosen = []
+    for lo, hi, js, cond in (
+        (first_half, n, range(0, turn), me < first_half),
+        (0, first_half, range(turn + 1, n - 1), me >= first_half),
+    ):
+        for j in js:
+            pk_waits[j].wait_recv()
+
+        @pl.when(cond)
+        def _():
+            pk_waits[turn].wait_recv()
+
+        hots = choose(pk_in[lo:hi].reshape((hi - lo) * SUB, lanes))
+        chosen.append(hots)
+        for k in range(PARTS):
+            block = mm(hots[0], tok[:, front(k)]) + fold(hots[1:], tok[:, back(k)])
+            x_out[k, lo:hi] = block.astype(BF16).reshape(hi - lo, SUB, wide)
+            for j in js:
+                x_copies[k][j].start()
+
+            @pl.when(cond)
+            def _(k=k):
+                x_copies[k][turn].start()
+
+    for k in range(PARTS):
         x_in[k, me] = x_out[k, me]
-        for copy in x_copies[k]:
-            copy.start()
+    main, *tails = [jnp.concatenate(hots, axis=0) for hots in zip(*chosen[::-1])]
 
     gate_act = up_act = logits = None
 
@@ -165,7 +198,7 @@
     for k in range(PARTS):
         load_wg[k].wait()
         load_wu[k].wait()
-        for copy in x_copies[k]:
+        for copy in x_waits[k]:
             copy.wait_recv()
         x = x_in[k].reshape(rows, wide)
         x = jnp.concatenate([x, unfold(mm, spread, x).astype(BF16)], axis=1)
@@ -181,7 +214,7 @@
     load_wd.wait()
     y_copies = [
         [
-            send(y_out.at[k, peer], y_in.at[k, me], y_send.at[k, i], y_recv.at[k, i], peer)
+            send(y_out.at[k, peer], y_in.at[k, me], y_send.at[k, peer], y_recv.at[k, me], peer)
             for i, peer in enumerate(peers)
         ]
         for k in range(PARTS)
@@ -191,11 +224,18 @@
         block = jnp.where(row_sub < MOST, block[:, :wide], fold(gather, block[:, wide:].astype(BF16)))
         y_out[k] = block.astype(BF16).reshape(n, SUB, wide)
         y_in[k, me] = y_out[k, me]
-        for copy in y_copies[k]:
+        for copy in y_copies[k][::-1]:
             copy.start()
 
-    for k in range(PARTS):
-        for copy in y_copies[k]:
+    y_waits = [
+        [
+            send(y_out.at[k, peer], y_in.at[k, peer], y_send.at[k, peer], y_recv.at[k, peer], peer)
+            for i, peer in enumerate(peers)
+        ]
+        for k in range(PARTS)
+    ]
+    for k in range(PARTS):
+        for copy in y_waits[k]:
             copy.wait_recv()
         y = y_in[k].reshape(rows, wide)
         out[:, front(k)] = mm_t(main, y).astype(BF16)
@@ -216,7 +256,7 @@
     dma = pltpu.SemaphoreType.DMA
     block = pltpu.VMEM((PARTS, n, SUB, wide), BF16)
     return pl.pallas_call(
-        functools.partial(kernel, n),
+        functools.partial(kernel, n, n // 2),
         out_shape=pltpu.VMEM((tok_dev, width), BF16),
         in_specs=[pl.BlockSpec(memory_space=pl.ANY)] * 6,
         out_specs=pl.BlockSpec(memory_space=pltpu.VMEM),
@@ -231,9 +271,9 @@
             pltpu.VMEM((n, SUB, lanes), jnp.int32),
             block, block, block, block,
             dma((4,)), dma((PARTS,)), dma((PARTS,)),
-            dma((n - 1,)), dma((n - 1,)),
-            dma((PARTS, n - 1)), dma((PARTS, n - 1)),
-            dma((PARTS, n - 1)), dma((PARTS, n - 1)),
+            dma((n,)), dma((n,)),
+            dma((PARTS, n)), dma((PARTS, n)),
+            dma((PARTS, n)), dma((PARTS, n)),
         ],
         compiler_params=pltpu.CompilerParams(collective_id=0, has_side_effects=True),
     )(tokens, router.T, w_gate, w_up, w_down, picks)

time: 24.6 us -> 23.9 us (0.972)
  Pallas kernels: 23.5 us -> 22.7 us
    pallas_call x1, Pallas kernels: 23.5 us -> 22.7 us  [body(): pl.pallas_call(functools.partial(kernel, n, n // 2), out_shape=pltpu.VMEM...]
where the time goes in v1:
time: 23.9 us; the launch traced here: 23.7 us
  Pallas kernels  22.7 us (95%)
  local copies, waits for them, and re-layouts  0.97 us (4%)
    pallas_call x1, Pallas kernels, body(): pl.pallas_call(functools.partial(kernel, n, n // 2), out_shape=pltpu.VMEM...  22.7 us
    unnamed x1, local copies, waits for them, and re-layouts  0.97 us

profile of v1, /device:TPU:0, one launch (start us, length us, event | category | flops | bytes accessed | tf_op | source)
XLA Modules:
  0.0 23.7 jit_solution(366456812849938602)
XLA Ops:
  0.0 22.7 %shard_map.64 = bf16[256,2048]{1,0:T(8,128)(2,1)S(1)} custom-call(bf16[256,2048]{1,0:T(8,128)(2,1)} %tokens.1, bf16[8,2048]{1,0:T(8,128)(2,1)} %bitcast.1, bf16[1,2048,768]{2,1,0:T(8,128)(2,1)} %w_gate.1, bf16[1,2048,768]{2,1,0:T(8,128)(2,1)} %w_up.1, bf16[1,768,2048]{2,1,0:T(8,128)(2,1)} %w_down.1, s32[1,32]{1,0:T(1,128)} %picks.1), custom_call_target="tpu_custom_call" | custom-call | tf_op jit(solution)/shard_map/pallas_call | solution.py:258
  22.7 1.0 %copy.8 = bf16[256,2048]{1,0:T(8,128)(2,1)} copy(bf16[256,2048]{1,0:T(8,128)(2,1)S(1)} %shard_map.64) | data formatting | bytes 2097152

commit v2 on v0

v2 whole, which is shorter than its diff:
```python
import functools

import jax
import jax.numpy as jnp
from jax import lax
from jax.experimental import pallas as pl
from jax.experimental.pallas import tpu as pltpu
from jax.sharding import PartitionSpec as P

MESH = pl.DeviceIdType.MESH
PAIRS = 3
LOADS = 4
X_PARTS = 2
Y_PARTS = 2
F32 = jnp.float32
BF16 = jnp.bfloat16


def mm(a, b):
    return jnp.dot(a, b, preferred_element_type=F32)


def mm_t(a, b):
    return lax.dot_general(a, b, (((0,), (0,)), ((), ())), preferred_element_type=F32)


def kernel(
    n, tokens, router, w_gate, w_up, w_down, picks, out,
    tok, rout, wg, wu, wd, pk_own, pk_out, pk_in, x_out, x_in, y_out, y_in,
    load_sem, wg_sem, wu_sem,
    pk_send, pk_recv, x_send, x_recv, y_send, y_recv,
):
    me = lax.axis_index("dp")
    tok_dev, width = tok.shape
    cap = picks.shape[1]
    lanes = pk_out.shape[1]
    experts = rout.shape[0]
    half = n // 2

    def span(k, parts):
        return pl.ds(k * (width // parts), width // parts)

    def rows_of(ref):
        groups = [ref[:, i].reshape(2 * n, ref.shape[-1]) for i in range(PAIRS)]
        return jnp.concatenate(groups, axis=0)

    load_tok = pltpu.make_async_copy(tokens, tok, load_sem.at[0])
    load_rout = pltpu.make_async_copy(router, rout, load_sem.at[1])
    load_pk = pltpu.make_async_copy(picks, pk_own, load_sem.at[3])
    load_wd = pltpu.make_async_copy(w_down.at[0], wd, load_sem.at[2])
    load_wg = [
        pltpu.make_async_copy(w_gate.at[0, span(k, LOADS)], wg.at[span(k, LOADS)], wg_sem.at[k])
        for k in range(LOADS)
    ]
    load_wu = [
        pltpu.make_async_copy(w_up.at[0, span(k, LOADS)], wu.at[span(k, LOADS)], wu_sem.at[k])
        for k in range(LOADS)
    ]

    barrier = pltpu.get_barrier_semaphore()
    peers = [n - 1 - j - (n - 1 - j <= me).astype(jnp.int32) for j in range(n - 1)]
    for peer in peers:
        pl.semaphore_signal(barrier, inc=1, device_id={"dp": peer}, device_id_type=MESH)
    load_pk.start()
    load_tok.start()
    load_rout.start()
    for k in range(LOADS):
        load_wg[k].start()
        load_wu[k].start()
    load_wd.start()

    pk_out[...] = jnp.full((2, lanes), 1 << 30, jnp.int32)
    load_pk.wait()
    pk_out[:, pl.ds(0, cap)] = jnp.broadcast_to(pk_own[...], (2, cap))
    pk_in[me] = pk_out[...]
    pl.semaphore_wait(barrier, n - 1)

    def copy_of(src, dst, send_sem, recv_sem, peer):
        return pltpu.make_async_remote_copy(
            src_ref=src, dst_ref=dst, send_sem=send_sem, recv_sem=recv_sem,
            device_id={"dp": peer}, device_id_type=MESH,
        )

    def exchange(src, dst, send_sem, recv_sem):
        puts = [copy_of(src.at[p], dst.at[me], send_sem.at[p], recv_sem.at[me], p) for p in peers]
        gets = [copy_of(src.at[p], dst.at[p], send_sem.at[p], recv_sem.at[p], p) for p in peers]
        return puts, gets

    pk_puts = [copy_of(pk_out, pk_in.at[me], pk_send.at[p], pk_recv.at[me], p) for p in peers]
    pk_gets = [copy_of(pk_out, pk_in.at[p], pk_send.at[p], pk_recv.at[p], p) for p in peers]
    for put in pk_puts:
        put.start()

    load_tok.wait()
    load_rout.wait()
    logits = lax.dot_general(
        rout[...], tok[...], (((1,), (1,)), ((), ())), preferred_element_type=F32
    )
    e = jnp.exp(logits - jnp.max(logits, axis=0, keepdims=True))
    gates = (experts * (e / jnp.sum(e, axis=0, keepdims=True))).astype(BF16).astype(F32)

    low = me * tok_dev

    def choose(first, last):
        pk = pk_in[first:last].reshape(2 * (last - first), lanes)
        pk = jnp.concatenate([pk] * PAIRS, axis=0)
        count = pk.shape[0]
        mine = (pk >= low) & (pk < low + tok_dev)
        start = jnp.sum(jnp.where(pk < low, 1.0, 0.0), axis=1, keepdims=True).astype(jnp.int32)
        slot = lax.broadcasted_iota(jnp.int32, (count, lanes), 1) - start
        place = (pk - low + 1).astype(F32)
        row = lax.broadcasted_iota(jnp.int32, (count, 1), 0)
        want = 2 * (row // (count // PAIRS)) + row % 2
        at = jnp.sum(jnp.where(mine & (slot == want), place, 0.0), axis=1, keepdims=True)
        token_at = lax.broadcasted_iota(jnp.int32, (count, tok_dev), 1).astype(F32) + 1.0
        return jnp.where(token_at == at, 1.0, 0.0)

    x_puts, x_gets = zip(*[
        exchange(x_out.at[k], x_in.at[k], x_send.at[k], x_recv.at[k]) for k in range(X_PARTS)
    ])
    y_puts, y_gets = zip(*[
        exchange(y_out.at[k], y_in.at[k], y_send.at[k], y_recv.at[k]) for k in range(Y_PARTS)
    ])
    turn = half - 1
    for first, last, js, also in (
        (n - half, n, range(turn), me < n - half),
        (0, n - half, range(turn + 1, n - 1), me >= n - half),
    ):
        for j in js:
            pk_gets[j].wait_recv()

        @pl.when(also)
        def _():
            pk_gets[turn].wait_recv()

        size = 2 * (last - first)
        hot = choose(first, last).astype(BF16)
        for k in range(X_PARTS):
            block = mm(hot, tok[:, span(k, X_PARTS)])
            for i in range(PAIRS):
                rows = block[i * size : (i + 1) * size].astype(BF16)
                x_out[k, first:last, i] = rows.reshape(last - first, 2, rows.shape[1])
            for j in js:
                x_puts[k][j].start()

            @pl.when(also)
            def _(k=k):
                x_puts[k][turn].start()

    for k in range(X_PARTS):
        x_in[k, me] = x_out[k, me]
    gate_of = jnp.broadcast_to(gates[:, None, :], (n, 2, tok_dev)).reshape(2 * n, tok_dev)
    spread = (choose(0, n) * jnp.concatenate([gate_of] * PAIRS, axis=0)).T.astype(BF16)

    for copy in load_wg + load_wu:
        copy.wait()
    gate_act = up_act = None
    for k in range(X_PARTS):
        for get in x_gets[k]:
            get.wait_recv()
        x = rows_of(x_in.at[k])
        gate_part = mm(x, wg[span(k, X_PARTS)])
        up_part = mm(x, wu[span(k, X_PARTS)])
        gate_act = gate_part if k == 0 else gate_act + gate_part
        up_act = up_part if k == 0 else up_act + up_part
    hidden = (gate_act / (1.0 + jnp.exp(-gate_act)) * up_act).astype(BF16)

    load_wd.wait()
    for k in range(Y_PARTS):
        block = mm(hidden, wd[:, span(k, Y_PARTS)]).astype(BF16)
        for i in range(PAIRS):
            rows = block[i * 2 * n : (i + 1) * 2 * n]
            y_out[k, :, i] = rows.reshape(n, 2, rows.shape[1])
        for put in y_puts[k][::-1][:1]:
            put.start()
        y_in[k, me] = y_out[k, me]
    for k in range(Y_PARTS):
        for put in y_puts[k][::-1][1:]:
            put.start()

    for puts in [pk_puts, *x_puts]:
        for put in puts:
            put.wait_send()
    for k in range(Y_PARTS):
        for get in y_gets[k]:
            get.wait_recv()
        out[:, span(k, Y_PARTS)] = mm(spread, rows_of(y_in.at[k])).astype(BF16)
    for puts in y_puts:
        for put in puts:
            put.wait_send()


def body(tokens, router, w_gate, w_up, w_down, picks):
    n = lax.axis_size("dp")
    tok_dev, width = tokens.shape
    hidden = w_gate.shape[2]
    cap = picks.shape[1]
    lanes = -(-cap // 128) * 128
    experts = router.shape[1]
    dma = pltpu.SemaphoreType.DMA
    x_block = pltpu.VMEM((X_PARTS, n, PAIRS, 2, width // X_PARTS), BF16)
    y_block = pltpu.VMEM((Y_PARTS, n, PAIRS, 2, width // Y_PARTS), BF16)
    return pl.pallas_call(
        functools.partial(kernel, n),
        out_shape=pltpu.VMEM((tok_dev, width), BF16),
        in_specs=[pl.BlockSpec(memory_space=pl.ANY)] * 6,
        out_specs=pl.BlockSpec(memory_space=pltpu.VMEM),
        scratch_shapes=[
            pltpu.VMEM((tok_dev, width), BF16),
            pltpu.VMEM((experts, width), BF16),
            pltpu.VMEM((width, hidden), BF16),
            pltpu.VMEM((width, hidden), BF16),
            pltpu.VMEM((hidden, width), BF16),
            pltpu.VMEM((1, cap), jnp.int32),
            pltpu.VMEM((2, lanes), jnp.int32),
            pltpu.VMEM((n, 2, lanes), jnp.int32),
            x_block, x_block, y_block, y_block,
            dma((4,)), dma((LOADS,)), dma((LOADS,)),
            dma((n,)), dma((n,)),
            dma((X_PARTS, n)), dma((X_PARTS, n)),
            dma((Y_PARTS, n)), dma((Y_PARTS, n)),
        ],
        compiler_params=pltpu.CompilerParams(collective_id=0, has_side_effects=True),
    )(tokens, router.T, w_gate, w_up, w_down, picks)


def solution(mesh):
    return jax.shard_map(
        body,
        mesh=mesh,
        in_specs=(
            P(("rep", "dp"), None),
            P("rep", None),
            P("dp", None, None),
            P("dp", None, None),
            P("dp", None, None),
            P(("rep", "dp"), None),
        ),
        out_specs=P(("rep", "dp"), None),
        check_vma=False,
    )
```

time: 24.6 us -> 22.6 us (0.919)
  Pallas kernels: 23.5 us -> 21.4 us
    pallas_call x1, Pallas kernels: 23.5 us -> 21.4 us  [body(): pl.pallas_call(functools.partial(kernel, n), out_shape=pltpu.VMEM((tok_de...]
where the time goes in v2:
time: 22.6 us; the launch traced here: 22.4 us
  Pallas kernels  21.4 us (95%)
  local copies, waits for them, and re-layouts  0.97 us (4%)
    pallas_call x1, Pallas kernels, body(): pl.pallas_call(functools.partial(kernel, n), out_shape=pltpu.VMEM((tok_de...  21.4 us
    unnamed x1, local copies, waits for them, and re-layouts  0.97 us

profile of v2, /device:TPU:0, one launch (start us, length us, event | category | flops | bytes accessed | tf_op | source)
XLA Modules:
  0.0 22.4 jit_solution(3564110702831393334)
XLA Ops:
  0.0 21.4 %shard_map.64 = bf16[256,2048]{1,0:T(8,128)(2,1)S(1)} custom-call(bf16[256,2048]{1,0:T(8,128)(2,1)} %tokens.1, bf16[8,2048]{1,0:T(8,128)(2,1)} %bitcast.1, bf16[1,2048,768]{2,1,0:T(8,128)(2,1)} %w_gate.1, bf16[1,2048,768]{2,1,0:T(8,128)(2,1)} %w_up.1, bf16[1,768,2048]{2,1,0:T(8,128)(2,1)} %w_down.1, s32[1,32]{1,0:T(1,128)} %picks.1), custom_call_target="tpu_custom_call" | custom-call | tf_op jit(solution)/shard_map/pallas_call | solution.py:203
  21.4 1.0 %copy.8 = bf16[256,2048]{1,0:T(8,128)(2,1)} copy(bf16[256,2048]{1,0:T(8,128)(2,1)S(1)} %shard_map.64) | data formatting | bytes 2097152

commit v3 on v2

--- a/solution.py
+++ b/solution.py
@@ -41,7 +41,7 @@
         return pl.ds(k * (width // parts), width // parts)
 
     def rows_of(ref):
-        groups = [ref[:, i].reshape(2 * n, ref.shape[-1]) for i in range(PAIRS)]
+        groups = [ref[:, i].reshape(2 * ref.shape[0], ref.shape[-1]) for i in range(PAIRS)]
         return jnp.concatenate(groups, axis=0)
 
     load_tok = pltpu.make_async_copy(tokens, tok, load_sem.at[0])
@@ -122,10 +122,11 @@
         exchange(y_out.at[k], y_in.at[k], y_send.at[k], y_recv.at[k]) for k in range(Y_PARTS)
     ])
     turn = half - 1
-    for first, last, js, also in (
+    sides = (
         (n - half, n, range(turn), me < n - half),
         (0, n - half, range(turn + 1, n - 1), me >= n - half),
-    ):
+    )
+    for first, last, js, also in sides:
         for j in js:
             pk_gets[j].wait_recv()
 
@@ -154,29 +155,38 @@
 
     for copy in load_wg + load_wu:
         copy.wait()
-    gate_act = up_act = None
-    for k in range(X_PARTS):
-        for get in x_gets[k]:
-            get.wait_recv()
-        x = rows_of(x_in.at[k])
-        gate_part = mm(x, wg[span(k, X_PARTS)])
-        up_part = mm(x, wu[span(k, X_PARTS)])
-        gate_act = gate_part if k == 0 else gate_act + gate_part
-        up_act = up_part if k == 0 else up_act + up_part
-    hidden = (gate_act / (1.0 + jnp.exp(-gate_act)) * up_act).astype(BF16)
-
     load_wd.wait()
+    for first, last, js, also in sides[::-1]:
+        size = 2 * (last - first)
+        gate_act = up_act = None
+        for k in range(X_PARTS):
+            for j in js:
+                x_gets[k][j].wait_recv()
+
+            @pl.when(also)
+            def _(k=k):
+                x_gets[k][turn].wait_recv()
+
+            x = rows_of(x_in.at[k, first:last])
+            gate_part = mm(x, wg[span(k, X_PARTS)])
+            up_part = mm(x, wu[span(k, X_PARTS)])
+            gate_act = gate_part if k == 0 else gate_act + gate_part
+            up_act = up_part if k == 0 else up_act + up_part
+        hidden = (gate_act / (1.0 + jnp.exp(-gate_act)) * up_act).astype(BF16)
+        for k in range(Y_PARTS):
+            block = mm(hidden, wd[:, span(k, Y_PARTS)])
+            for i in range(PAIRS):
+                rows = block[i * size : (i + 1) * size].astype(BF16)
+                y_out[k, first:last, i] = rows.reshape(last - first, 2, rows.shape[1])
+            for j in reversed(js):
+                y_puts[k][j].start()
+
+            @pl.when(also)
+            def _(k=k):
+                y_puts[k][turn].start()
+
     for k in range(Y_PARTS):
-        block = mm(hidden, wd[:, span(k, Y_PARTS)]).astype(BF16)
-        for i in range(PAIRS):
-            rows = block[i * 2 * n : (i + 1) * 2 * n]
-            y_out[k, :, i] = rows.reshape(n, 2, rows.shape[1])
-        for put in y_puts[k][::-1][:1]:
-            put.start()
         y_in[k, me] = y_out[k, me]
-    for k in range(Y_PARTS):
-        for put in y_puts[k][::-1][1:]:
-            put.start()
 
     for puts in [pk_puts, *x_puts]:
         for put in puts:

time: 22.6 us -> 22.2 us (0.982)
  Pallas kernels: 21.4 us -> 21 us
    pallas_call x1, Pallas kernels: 21.4 us -> 21 us  [body(): pl.pallas_call(functools.partial(kernel, n), out_shape=pltpu.VMEM((tok_de...]
where the time goes in v3:
time: 22.2 us; the launch traced here: 22 us
  Pallas kernels  21 us (95%)
  local copies, waits for them, and re-layouts  0.97 us (4%)
    pallas_call x1, Pallas kernels, body(): pl.pallas_call(functools.partial(kernel, n), out_shape=pltpu.VMEM((tok_de...  21 us
    unnamed x1, local copies, waits for them, and re-layouts  0.97 us

profile of v3, /device:TPU:0, one launch (start us, length us, event | category | flops | bytes accessed | tf_op | source)
XLA Modules:
  0.0 22.0 jit_solution(8644368771951409321)
XLA Ops:
  0.0 21.0 %shard_map.64 = bf16[256,2048]{1,0:T(8,128)(2,1)S(1)} custom-call(bf16[256,2048]{1,0:T(8,128)(2,1)} %tokens.1, bf16[8,2048]{1,0:T(8,128)(2,1)} %bitcast.1, bf16[1,2048,768]{2,1,0:T(8,128)(2,1)} %w_gate.1, bf16[1,2048,768]{2,1,0:T(8,128)(2,1)} %w_up.1, bf16[1,768,2048]{2,1,0:T(8,128)(2,1)} %w_down.1, s32[1,32]{1,0:T(1,128)} %picks.1), custom_call_target="tpu_custom_call" | custom-call | tf_op jit(solution)/shard_map/pallas_call | solution.py:213
  21.1 1.0 %copy.8 = bf16[256,2048]{1,0:T(8,128)(2,1)} copy(bf16[256,2048]{1,0:T(8,128)(2,1)S(1)} %shard_map.64) | data formatting | bytes 2097152

commit v4 on v3

--- a/solution.py
+++ b/solution.py
@@ -10,8 +10,10 @@
 MESH = pl.DeviceIdType.MESH
 PAIRS = 3
 LOADS = 4
-X_PARTS = 2
-Y_PARTS = 2
+X_CUTS = (0, 4, 8)
+Y_CUTS = (0, 4, 8)
+X_PARTS = len(X_CUTS) - 1
+Y_PARTS = len(Y_CUTS) - 1
 F32 = jnp.float32
 BF16 = jnp.bfloat16
 
@@ -40,8 +42,12 @@
     def span(k, parts):
         return pl.ds(k * (width // parts), width // parts)
 
-    def rows_of(ref):
-        groups = [ref[:, i].reshape(2 * ref.shape[0], ref.shape[-1]) for i in range(PAIRS)]
+    def cut(k, cuts):
+        unit = width // cuts[-1]
+        return pl.ds(cuts[k] * unit, (cuts[k + 1] - cuts[k]) * unit)
+
+    def rows_of(ref, cols):
+        groups = [ref[:, i, :, cols].reshape(2 * ref.shape[0], cols.size) for i in range(PAIRS)]
         return jnp.concatenate(groups, axis=0)
 
     load_tok = pltpu.make_async_copy(tokens, tok, load_sem.at[0])
@@ -81,10 +87,13 @@
             device_id={"dp": peer}, device_id_type=MESH,
         )
 
-    def exchange(src, dst, send_sem, recv_sem):
-        puts = [copy_of(src.at[p], dst.at[me], send_sem.at[p], recv_sem.at[me], p) for p in peers]
-        gets = [copy_of(src.at[p], dst.at[p], send_sem.at[p], recv_sem.at[p], p) for p in peers]
-        return puts, gets
+    def exchange(src, dst, send_sem, recv_sem, cols):
+        def copy(p, q):
+            return copy_of(
+                src.at[p, :, :, cols], dst.at[q, :, :, cols], send_sem.at[p], recv_sem.at[q], p
+            )
+
+        return [copy(p, me) for p in peers], [copy(p, p) for p in peers]
 
     pk_puts = [copy_of(pk_out, pk_in.at[me], pk_send.at[p], pk_recv.at[me], p) for p in peers]
     pk_gets = [copy_of(pk_out, pk_in.at[p], pk_send.at[p], pk_recv.at[p], p) for p in peers]
@@ -116,10 +125,10 @@
         return jnp.where(token_at == at, 1.0, 0.0)
 
     x_puts, x_gets = zip(*[
-        exchange(x_out.at[k], x_in.at[k], x_send.at[k], x_recv.at[k]) for k in range(X_PARTS)
+        exchange(x_out, x_in, x_send.at[k], x_recv.at[k], cut(k, X_CUTS)) for k in range(X_PARTS)
     ])
     y_puts, y_gets = zip(*[
-        exchange(y_out.at[k], y_in.at[k], y_send.at[k], y_recv.at[k]) for k in range(Y_PARTS)
+        exchange(y_out, y_in, y_send.at[k], y_recv.at[k], cut(k, Y_CUTS)) for k in range(Y_PARTS)
     ])
     turn = half - 1
     sides = (
@@ -137,10 +146,11 @@
         size = 2 * (last - first)
         hot = choose(first, last).astype(BF16)
         for k in range(X_PARTS):
-            block = mm(hot, tok[:, span(k, X_PARTS)])
+            cols = cut(k, X_CUTS)
+            block = mm(hot, tok[:, cols])
             for i in range(PAIRS):
                 rows = block[i * size : (i + 1) * size].astype(BF16)
-                x_out[k, first:last, i] = rows.reshape(last - first, 2, rows.shape[1])
+                x_out[first:last, i, :, cols] = rows.reshape(last - first, 2, rows.shape[1])
             for j in js:
                 x_puts[k][j].start()
 
@@ -148,8 +158,7 @@
             def _(k=k):
                 x_puts[k][turn].start()
 
-    for k in range(X_PARTS):
-        x_in[k, me] = x_out[k, me]
+    x_in[me] = x_out[me]
     gate_of = jnp.broadcast_to(gates[:, None, :], (n, 2, tok_dev)).reshape(2 * n, tok_dev)
     spread = (choose(0, n) * jnp.concatenate([gate_of] * PAIRS, axis=0)).T.astype(BF16)
 
@@ -167,26 +176,31 @@
             def _(k=k):
                 x_gets[k][turn].wait_recv()
 
-            x = rows_of(x_in.at[k, first:last])
-            gate_part = mm(x, wg[span(k, X_PARTS)])
-            up_part = mm(x, wu[span(k, X_PARTS)])
+            cols = cut(k, X_CUTS)
+            x = rows_of(x_in.at[first:last], cols)
+            gate_part = mm(x, wg[cols])
+            up_part = mm(x, wu[cols])
             gate_act = gate_part if k == 0 else gate_act + gate_part
             up_act = up_part if k == 0 else up_act + up_part
         hidden = (gate_act / (1.0 + jnp.exp(-gate_act)) * up_act).astype(BF16)
         for k in range(Y_PARTS):
-            block = mm(hidden, wd[:, span(k, Y_PARTS)])
+            cols = cut(k, Y_CUTS)
+            block = mm(hidden, wd[:, cols])
             for i in range(PAIRS):
                 rows = block[i * size : (i + 1) * size].astype(BF16)
-                y_out[k, first:last, i] = rows.reshape(last - first, 2, rows.shape[1])
-            for j in reversed(js):
+                y_out[first:last, i, :, cols] = rows.reshape(last - first, 2, rows.shape[1])
+            for j in list(reversed(js))[:2]:
+                y_puts[k][j].start()
+
+        for k in range(Y_PARTS):
+            for j in list(reversed(js))[2:]:
                 y_puts[k][j].start()
 
             @pl.when(also)
             def _(k=k):
                 y_puts[k][turn].start()
 
-    for k in range(Y_PARTS):
-        y_in[k, me] = y_out[k, me]
+    y_in[me] = y_out[me]
 
     for puts in [pk_puts, *x_puts]:
         for put in puts:
@@ -194,7 +208,8 @@
     for k in range(Y_PARTS):
         for get in y_gets[k]:
             get.wait_recv()
-        out[:, span(k, Y_PARTS)] = mm(spread, rows_of(y_in.at[k])).astype(BF16)
+        cols = cut(k, Y_CUTS)
+        out[:, cols] = mm(spread, rows_of(y_in, cols)).astype(BF16)
     for puts in y_puts:
         for put in puts:
             put.wait_send()
@@ -208,8 +223,7 @@
     lanes = -(-cap // 128) * 128
     experts = router.shape[1]
     dma = pltpu.SemaphoreType.DMA
-    x_block = pltpu.VMEM((X_PARTS, n, PAIRS, 2, width // X_PARTS), BF16)
-    y_block = pltpu.VMEM((Y_PARTS, n, PAIRS, 2, width // Y_PARTS), BF16)
+    block = pltpu.VMEM((n, PAIRS, 2, width), BF16)
     return pl.pallas_call(
         functools.partial(kernel, n),
         out_shape=pltpu.VMEM((tok_dev, width), BF16),
@@ -224,7 +238,7 @@
             pltpu.VMEM((1, cap), jnp.int32),
             pltpu.VMEM((2, lanes), jnp.int32),
             pltpu.VMEM((n, 2, lanes), jnp.int32),
-            x_block, x_block, y_block, y_block,
+            block, block, block, block,
             dma((4,)), dma((LOADS,)), dma((LOADS,)),
             dma((n,)), dma((n,)),
             dma((X_PARTS, n)), dma((X_PARTS, n)),

time: 22.2 us -> 21.9 us (0.986)
    pallas_call x1, Pallas kernels: 21 us -> 20.8 us  [body(): pl.pallas_call(functools.partial(kernel, n), out_shape=pltpu.VMEM((tok_de...]
where the time goes in v4:
time: 21.9 us; the launch traced here: 21.8 us
  Pallas kernels  20.8 us (95%)
  local copies, waits for them, and re-layouts  0.97 us (4%)
    pallas_call x1, Pallas kernels, body(): pl.pallas_call(functools.partial(kernel, n), out_shape=pltpu.VMEM((tok_de...  20.8 us
    unnamed x1, local copies, waits for them, and re-layouts  0.97 us

profile of v4, /device:TPU:0, one launch (start us, length us, event | category | flops | bytes accessed | tf_op | source)
XLA Modules:
  0.0 21.8 jit_solution(9480092414201718845)
XLA Ops:
  0.0 20.8 %shard_map.64 = bf16[256,2048]{1,0:T(8,128)(2,1)S(1)} custom-call(bf16[256,2048]{1,0:T(8,128)(2,1)} %tokens.1, bf16[8,2048]{1,0:T(8,128)(2,1)} %bitcast.1, bf16[1,2048,768]{2,1,0:T(8,128)(2,1)} %w_gate.1, bf16[1,2048,768]{2,1,0:T(8,128)(2,1)} %w_up.1, bf16[1,768,2048]{2,1,0:T(8,128)(2,1)} %w_down.1, s32[1,32]{1,0:T(1,128)} %picks.1), custom_call_target="tpu_custom_call" | custom-call | tf_op jit(solution)/shard_map/pallas_call | solution.py:227
  20.8 1.0 %copy.8 = bf16[256,2048]{1,0:T(8,128)(2,1)} copy(bf16[256,2048]{1,0:T(8,128)(2,1)S(1)} %shard_map.64) | data formatting | bytes 2097152

commit v5 on v4

--- a/solution.py
+++ b/solution.py
@@ -63,11 +63,11 @@
         for k in range(LOADS)
     ]
 
+    load_pk.start()
     barrier = pltpu.get_barrier_semaphore()
     peers = [n - 1 - j - (n - 1 - j <= me).astype(jnp.int32) for j in range(n - 1)]
     for peer in peers:
         pl.semaphore_signal(barrier, inc=1, device_id={"dp": peer}, device_id_type=MESH)
-    load_pk.start()
     load_tok.start()
     load_rout.start()
     for k in range(LOADS):
@@ -183,22 +183,25 @@
             gate_act = gate_part if k == 0 else gate_act + gate_part
             up_act = up_part if k == 0 else up_act + up_part
         hidden = (gate_act / (1.0 + jnp.exp(-gate_act)) * up_act).astype(BF16)
+        order = [*reversed(js)]
+        order = [turn, *order] if first else [*order, turn]
+
+        def put(k, some):
+            for j in some:
+                if j in js:
+                    y_puts[k][j].start()
+                else:
+                    pl.when(also)(y_puts[k][j].start)
+
         for k in range(Y_PARTS):
             cols = cut(k, Y_CUTS)
             block = mm(hidden, wd[:, cols])
             for i in range(PAIRS):
                 rows = block[i * size : (i + 1) * size].astype(BF16)
                 y_out[first:last, i, :, cols] = rows.reshape(last - first, 2, rows.shape[1])
-            for j in list(reversed(js))[:2]:
-                y_puts[k][j].start()
-
+            put(k, order[:2])
         for k in range(Y_PARTS):
-            for j in list(reversed(js))[2:]:
-                y_puts[k][j].start()
-
-            @pl.when(also)
-            def _(k=k):
-                y_puts[k][turn].start()
+            put(k, order[2:])
 
     y_in[me] = y_out[me]
 

time: 21.9 us -> 21.9 us (level)
  no operation moved by 1% of the time
where the time goes in v5:
time: 21.9 us; the launch traced here: 21.8 us
  Pallas kernels  20.8 us (95%)
  local copies, waits for them, and re-layouts  0.97 us (4%)
    pallas_call x1, Pallas kernels, body(): pl.pallas_call(functools.partial(kernel, n), out_shape=pltpu.VMEM((tok_de...  20.8 us
    unnamed x1, local copies, waits for them, and re-layouts  0.97 us

profile of v5, /device:TPU:0, one launch (start us, length us, event | category | flops | bytes accessed | tf_op | source)
XLA Modules:
  0.0 21.8 jit_solution(14444971519296785874)
XLA Ops:
  0.0 20.8 %shard_map.64 = bf16[256,2048]{1,0:T(8,128)(2,1)S(1)} custom-call(bf16[256,2048]{1,0:T(8,128)(2,1)} %tokens.1, bf16[8,2048]{1,0:T(8,128)(2,1)} %bitcast.1, bf16[1,2048,768]{2,1,0:T(8,128)(2,1)} %w_gate.1, bf16[1,2048,768]{2,1,0:T(8,128)(2,1)} %w_up.1, bf16[1,768,2048]{2,1,0:T(8,128)(2,1)} %w_down.1, s32[1,32]{1,0:T(1,128)} %picks.1), custom_call_target="tpu_custom_call" | custom-call | tf_op jit(solution)/shard_map/pallas_call | solution.py:230
  20.8 1.0 %copy.8 = bf16[256,2048]{1,0:T(8,128)(2,1)} copy(bf16[256,2048]{1,0:T(8,128)(2,1)S(1)} %shard_map.64) | data formatting | bytes 2097152
